TPU v7x, 32 devices: a whole 2x2x4 slice. The times are simulated.
32 devices in a mesh: ctx: 16 (over z, x, core), tp: 2 (over y).
Axes of the slice: x: 2, y: 2, z: 4, core: 2. Of those that a mesh axis runs over, the one named last changes fastest.
Arguments:
- queries: bfloat16 [4096, 12288], P(('ctx', 'tp')), may hold values from -64 to 64
- keys: bfloat16 [4096, 1024], P(('ctx', 'tp')), may hold values from -4 to 4
- values: bfloat16 [4096, 1024], P(('ctx', 'tp')), may hold values from -6 to 6
- block_order: int32 [16], replicated, may hold values from 0 to 15, each once
Outputs:
- attended: bfloat16 [4096, 12288], P(('ctx', 'tp'))
Inputs may be any that keep to these rules, and one draw needn't show every extreme that they name: A permutation: block r holds sequence span block_order[r] in its first 128 rows and span 2 * 16 - 1 - block_order[r] in its last 128 rows.
All inputs are finite; a program needn't handle non-finite values.
Results may differ from a plain program's by a relative error of at most 0.003.
Values may be sent and summed in bfloat16 or wider, within the bound.
No kernel may reach another device: no remote copies, remote signals or barrier semaphores. Data moves between devices by JAX's collectives and lax.ppermute only.
A program may use at most 128 MiB of HBM per device.

v0:
```python
import math

import jax
import jax.numpy as jnp
from jax import lax
from jax.sharding import PartitionSpec as P

HD = 128
PREV = 3


MASKED_SCORE = -1e30


def passed_along(value, axis, steps):
    count = lax.axis_size(axis)
    pairs = [(source, (source + steps) % count) for source in range(count)]
    return lax.ppermute(value, axis, pairs)


def block_positions(block_order, block_index, first_row, count, span_rows):
    block_total = block_order.shape[0]
    leading = jnp.sum(
        jnp.where(jnp.arange(block_total, dtype=jnp.int32) == block_index, block_order, 0)
    )
    row_ids = first_row + jnp.arange(count, dtype=jnp.int32)
    return jnp.where(
        row_ids < span_rows,
        leading * span_rows + row_ids,
        (2 * block_total - 1 - leading) * span_rows + row_ids - span_rows,
    )


def update(carried, queries_h, query_pos, key_part, value_part, key_pos):
    piece_rows = key_part.shape[0]
    block_rows = math.gcd(piece_rows, 256)
    block_count = piece_rows // block_rows
    score_scale = 1.0 / math.sqrt(queries_h.shape[-1])
    key_blocks = key_part.reshape(block_count, block_rows, key_part.shape[1], key_part.shape[2])
    value_blocks = value_part.reshape(
        block_count, block_rows, value_part.shape[1], value_part.shape[2]
    )
    pos_blocks = key_pos.reshape(block_count, block_rows)

    def advance(running, blocks_in):
        running_max, running_sum, numerator = running
        key_block, value_block, pos_block = blocks_in
        scores = (
            jnp.einsum("tkgd,skd->tkgs", queries_h, key_block, preferred_element_type=jnp.float32)
            * score_scale
        )
        visible = pos_block[None, None, None, :] <= query_pos[:, None, None, None]
        block_max = jnp.max(jnp.where(visible, scores, MASKED_SCORE), axis=-1)
        new_max = jnp.maximum(running_max, block_max)
        exp_scores = jnp.where(visible, jnp.exp(scores - new_max[..., None]), 0.0)
        rescale = jnp.exp(running_max - new_max)
        running_sum = running_sum * rescale + jnp.sum(exp_scores, axis=-1)
        weights = exp_scores.astype(jnp.bfloat16)
        numerator = numerator * rescale[..., None] + jnp.einsum(
            "tkgs,skd->tkgd", weights, value_block, preferred_element_type=jnp.float32
        )
        return ((new_max, running_sum, numerator), None)

    final_state, _ = lax.scan(advance, carried, (key_blocks, value_blocks, pos_blocks))
    return final_state


def per_device(queries, keys, values, block_order):
    block_total = block_order.shape[0]
    ctx_index = lax.axis_index("ctx")
    local_k, local_v = (
        lax.all_gather(keys, "tp", axis=0, tiled=True),
        lax.all_gather(values, "tp", axis=0, tiled=True),
    )
    first_row = lax.axis_index("tp") * queries.shape[0]
    token_rows = queries.shape[0]
    block_rows = local_k.shape[0]
    span_rows = block_rows // 2
    kv_local = local_k.shape[1] // HD
    group_size = queries.shape[1] // (HD * kv_local)
    queries_h = queries.reshape(token_rows, kv_local, group_size, HD)
    query_pos = block_positions(block_order, ctx_index, first_row, token_rows, span_rows)
    own_pair = jnp.stack(
        [local_k.reshape(block_rows, kv_local, HD), local_v.reshape(block_rows, kv_local, HD)]
    )
    state = (
        jnp.full((token_rows, kv_local, group_size), MASKED_SCORE, jnp.float32),
        jnp.zeros((token_rows, kv_local, group_size), jnp.float32),
        jnp.zeros((token_rows, kv_local, group_size, HD), jnp.float32),
    )
    own_pos = block_positions(block_order, ctx_index, 0, block_rows, span_rows)
    state = update(state, queries_h, query_pos, own_pair[0], own_pair[1], own_pos)
    moving = own_pair
    for step in range(1, PREV + 1):
        moving = passed_along(moving, "ctx", 1)
        source = (ctx_index - step) % block_total
        source_pos = block_positions(block_order, source, 0, block_rows, span_rows)
        state = update(state, queries_h, query_pos, moving[0], moving[1], source_pos)
    running_max, running_sum, numerator = state
    attended = (numerator / running_sum[..., None]).astype(jnp.bfloat16)
    attended = attended.reshape(token_rows, kv_local * group_size * HD)
    return attended


def solution(mesh):
    return jax.shard_map(
        per_device,
        mesh=mesh,
        in_specs=(P(("ctx", "tp"), None), P(("ctx", "tp"), None), P(("ctx", "tp"), None), P()),
        out_specs=P(("ctx", "tp"), None),
        check_vma=False,
    )
```

profile of v0, /device:TPU:0, one launch (start us, length us, event | category | flops | bytes accessed | tf_op | source)
XLA Modules:
  0.0 129.0 jit_solution(16622594366497145752)
XLA Ops:
  0.0 1.1 copy.18
  1.1 10.0 %all_gather.6 = bf16[256,1024]{0,1:T(8,128)(2,1)S(1)} all-gather(bf16[128,1024]{0,1:T(8,128)(2,1)S(1)} %copy.18), channel_id=1, replica_groups=mesh['ctx'=16,'tp'=2] {'tp'}, dimensions={0}, use_global_device_ids=true | all-gather | bytes 786432 | tf_op jit(solution)/shard_map/all_gather | solution.py:72
  11.1 1.3 copy.22
  12.4 8.2 %all_gather.7 = bf16[256,1024]{0,1:T(8,128)(2,1)S(1)} all-gather(bf16[128,1024]{0,1:T(8,128)(2,1)S(1)} %copy.22), channel_id=1, replica_groups=mesh['ctx'=16,'tp'=2] {'tp'}, dimensions={0}, use_global_device_ids=true | all-gather | bytes 786432 | tf_op jit(solution)/shard_map/all_gather | solution.py:73
  20.6 0.3 copy.25
  20.9 0.3 copy.24
  21.2 1.1 pad_maximum_fusion
  22.2 0.0 collective-permute-start
  22.2 1.4 %fusion.57 = (s32[]{:T(128)}, s32[]{:T(128)}, s32[]{:T(128)}, s32[]{:T(128)}) fusion(s32[16]{0:T(128)} %param.7, s32[]{:T(128)S(6)} %select_n.98, s32[]{:T(128)S(6)} %select_n.88, s32[]{:T(128)S(6)} %axis_index.23, s32[]{:T(128)S(6)} %select_n.93), kind=kLoop, calls=%fused_computation.90 | loop fusion | flops 188 | bytes 96 | tf_op jit(solution)/shard_map/reduce_sum | solution.py:23
  28.9 0.0 copy-done
  28.9 3.5 %copy.19 = bf16[128,12288]{0,1:T(8,128)(2,1)S(1)} copy(bf16[128,12288]{1,0:T(8,128)(2,1)} %param.4) | data formatting | bytes 6291456 | tf_op args[0]
  32.5 7.0 %collective-permute-done = bf16[2,256,8,128]{3,1,2,0:T(8,128)(2,1)} collective-permute-done((bf16[2,256,8,128]{3,1,2,0:T(8,128)(2,1)}, bf16[2,256,8,128]{3,1,2,0:T(8,128)(2,1)}, u32[]{:S(2)}, u32[]{:S(2)}) %collective-permute-start) | collective-permute-done | bytes 1048608 | tf_op jit(solution)/shard_map/ppermute | solution.py:18
  39.5 0.0 collective-permute-start.1
  39.5 0.2 broadcast_compare_fusion.3
  39.7 3.0 %fusion.9 = (f32[128,8,12]{0,2,1:T(8,128)S(1)}, f32[8,256,128,12]{2,1,3,0:T(8,128)S(1)}) fusion(pred[128,256]{0,1:T(8,128)(4,1)S(1)} %get-tuple-element.97, bf16[256,8,128,1]{0,2,3,1:T(8,128)(2,1)} %bitcast.152, bf16[128,8,12,128]{0,3,2,1:T(8,128)(2,1)S(1)} %bitcast.147), kind=kOutput, calls=%fused_computation.17 | convolution fusion | flops 814731264 | bytes 16334848 | tf_op jit(solution)/shard_map/while/body/eval_jaxpr/tkgd,skd->tkgs/dot_general | solution.py:49
  42.7 13.9 %collective-permute-done.1 = bf16[2,256,8,128]{3,1,2,0:T(8,128)(2,1)S(1)} collective-permute-done((bf16[2,256,8,128]{3,1,2,0:T(8,128)(2,1)}, bf16[2,256,8,128]{3,1,2,0:T(8,128)(2,1)S(1)}, u32[]{:S(2)}, u32[]{:S(2)}) %collective-permute-start.1) | collective-permute-done | bytes 1048608 | tf_op jit(solution)/shard_map/ppermute | solution.py:18
  56.6 0.0 collective-permute-start.2
  56.6 7.8 %fusion.6 = (f32[128,8,12]{0,2,1:T(8,128)S(1)}, f32[8,256,128,12]{2,1,3,0:T(8,128)}) fusion(pred[128,256]{0,1:T(8,128)(4,1)S(1)} %get-tuple-element.98, bf16[128,8,12,128]{0,3,2,1:T(8,128)(2,1)S(1)} %bitcast.148, bf16[2,256,8,128]{3,1,2,0:T(8,128)(2,1)} %collective-permute-done), kind=kOutput, calls=%fused_computation.12 | convolution fusion | flops 814731264 | bytes 16334848 | tf_op jit(solution)/shard_map/while/body/eval_jaxpr/tkgd,skd->tkgs/dot_general | solution.py:49
  64.4 1.9 %fusion.3 = (f32[128,8,12]{0,2,1:T(8,128)S(1)}, f32[8,256,128,12]{2,1,3,0:T(8,128)S(1)}) fusion(pred[128,256]{0,1:T(8,128)(4,1)S(1)} %get-tuple-element.108, bf16[128,8,12,128]{0,3,2,1:T(8,128)(2,1)S(1)} %bitcast.149, bf16[2,256,8,128]{3,1,2,0:T(8,128)(2,1)S(1)} %collective-permute-done.1), kind=kOutput, calls=%fused_computation.7 | convolution fusion | flops 814731264 | bytes 16334848 | tf_op jit(solution)/shard_map/while/body/eval_jaxpr/tkgd,skd->tkgs/dot_general | solution.py:49
  66.3 7.2 %collective-permute-done.2 = bf16[2,256,8,128]{3,1,2,0:T(8,128)(2,1)S(1)} collective-permute-done((bf16[2,256,8,128]{3,1,2,0:T(8,128)(2,1)S(1)}, bf16[2,256,8,128]{3,1,2,0:T(8,128)(2,1)S(1)}, u32[]{:S(2)}, u32[]{:S(2)}) %collective-permute-start.2) | collective-permute-done | bytes 1048608 | tf_op jit(solution)/shard_map/ppermute | solution.py:18
  73.5 6.4 %fusion = (f32[128,8,12]{0,2,1:T(8,128)S(1)}, f32[8,256,128,12]{2,1,3,0:T(8,128)}) fusion(pred[128,256]{0,1:T(8,128)(4,1)S(1)} %get-tuple-element.109, bf16[128,8,12,128]{0,3,2,1:T(8,128)(2,1)S(1)} %bitcast.150, bf16[2,256,8,128]{3,1,2,0:T(8,128)(2,1)S(1)} %collective-permute-done.2), kind=kOutput, calls=%fused_computation.2 | convolution fusion | flops 814731264 | bytes 16334848 | tf_op jit(solution)/shard_map/while/body/eval_jaxpr/tkgd,skd->tkgs/dot_general | solution.py:49
  80.0 4.5 %fusion.26 = f32[8,128,12,128]{1,3,2,0:T(8,128)} fusion(bf16[256,8,128,1]{0,2,3,1:T(8,128)(2,1)S(1)} %bitcast.156, f32[8,256,128,12]{2,1,3,0:T(8,128)S(1)} %get-tuple-element.126, f32[128,8,12]{0,2,1:T(8,128)S(1)} %get-tuple-element.96, pred[128,256]{0,1:T(8,128)(4,1)S(1)} %get-tuple-element.97), kind=kOutput, calls=%fused_computation.31 | convolution fusion | flops 817889280 | bytes 19480576 | tf_op jit(solution)/shard_map/while/body/eval_jaxpr/tkgs,skd->tkgd/dot_general | solution.py:59
  84.5 8.4 %fusion.12 = (f32[128,8,12]{0,2,1:T(8,128)S(1)}, f32[128,8,12]{0,2,1:T(8,128)S(1)}) fusion(f32[8,256,128,12]{2,1,3,0:T(8,128)S(1)} %get-tuple-element.126, f32[128,8,12]{0,2,1:T(8,128)S(1)} %get-tuple-element.96, pred[128,256]{0,1:T(8,128)(4,1)S(1)} %get-tuple-element.97, f32[128,8,12]{0,2,1:T(8,128)S(1)} %get-tuple-element.94, ...), kind=kLoop, calls=%fused_computation.20 | loop fusion | flops 25141248 | bytes 25427968 | tf_op jit(solution)/shard_map/while/body/eval_jaxpr/reduce_sum | solution.py:57
  92.9 8.4 %fusion.16 = (f32[128,8,12]{0,2,1:T(8,128)S(1)}, f32[128,8,12]{0,2,1:T(8,128)S(1)}) fusion(f32[8,256,128,12]{2,1,3,0:T(8,128)S(1)} %get-tuple-element.113, f32[128,8,12]{0,2,1:T(8,128)S(1)} %get-tuple-element.93, pred[128,256]{0,1:T(8,128)(4,1)S(1)} %get-tuple-element.108, f32[128,8,12]{0,2,1:T(8,128)S(1)} %get-tuple-element.92, ...), kind=kLoop, calls=%fused_computation.24 | loop fusion | flops 25141248 | bytes 25427968 | tf_op jit(solution)/shard_map/while/body/eval_jaxpr/reduce_sum | solution.py:57
  101.3 0.0 copy-start.4
  101.3 0.1 multiply_add_fusion
  101.3 0.0 slice-start
  101.4 10.0 %fusion.24 = f32[8,128,128,12]{2,1,3,0:T(8,128)} fusion(f32[8,256,128,12]{2,1,3,0:T(8,128)} %get-tuple-element.115, f32[128,8,12]{0,2,1:T(8,128)S(1)} %get-tuple-element.94, pred[128,256]{0,1:T(8,128)(4,1)S(1)} %get-tuple-element.98, bf16[2,256,8,128]{3,1,2,0:T(8,128)(2,1)} %collective-permute-done), kind=kOutput, calls=%fused_computation.30 | convolution fusion | flops 817889280 | bytes 19480576 | tf_op jit(solution)/shard_map/while/body/eval_jaxpr/tkgs,skd->tkgd/dot_general | solution.py:59
  111.4 0.0 copy-done.4
  111.4 4.2 %fusion.22 = f32[8,128,128,12]{2,1,3,0:T(8,128)} fusion(f32[8,256,128,12]{2,1,3,0:T(8,128)S(1)} %get-tuple-element.113, f32[128,8,12]{0,2,1:T(8,128)S(1)} %get-tuple-element.93, pred[128,256]{0,1:T(8,128)(4,1)S(1)} %get-tuple-element.108, bf16[2,256,8,128]{3,1,2,0:T(8,128)(2,1)S(1)} %copy-done.4), kind=kOutput, calls=%fused_computation.29 | convolution fusion | flops 817889280 | bytes 19496960 | tf_op jit(solution)/shard_map/while/body/eval_jaxpr/tkgs,skd->tkgd/dot_general | solution.py:59
  115.7 10.5 %fusion.29 = bf16[128,8,12,128]{0,3,2,1:T(8,128)(2,1)S(1)} fusion(f32[8,128,128,12]{2,1,3,0:T(8,128)} %fusion.22, f32[8,128,128,12]{2,1,3,0:T(8,128)} %fusion.24, f32[8,128,12,128]{1,3,2,0:T(8,128)S(1)} %bitcast.154, f32[128,8,12]{0,2,1:T(8,128)S(1)} %get-tuple-element.79, f32[128,8,12]{0,2,1:T(8,128)S(1)} %get-tuple-element.91, ...), kind=kOutput, calls=%fused_computation.34 | convolution fusion | flops 832045056 | bytes 35553280 | tf_op jit(solution)/shard_map/while/body/eval_jaxpr/tkgs,skd->tkgd/dot_general | solution.py:59
  126.2 2.8 %copy.35 = bf16[128,12288]{1,0:T(8,128)(2,1)} copy(bf16[128,12288]{0,1:T(8,128)(2,1)S(1)} %bitcast.157) | data formatting | bytes 6291456 | tf_op jit(solution)/shard_map/reshape | solution.py:101
  (21 shorter events, 0.1 us)
Async XLA Ops:
  11.1 17.8 %copy-start = (bf16[256,1024]{0,1:T(8,128)(2,1)}, bf16[256,1024]{0,1:T(8,128)(2,1)S(1)}, u32[]{:S(2)}) copy-start(bf16[256,1024]{0,1:T(8,128)(2,1)S(1)} %all_gather.6) | copy-start | bytes 1572868
  20.6 8.3 %copy-start.1 = (bf16[256,1024]{0,1:T(8,128)(2,1)}, bf16[256,1024]{0,1:T(8,128)(2,1)S(1)}, u32[]{:S(2)}) copy-start(bf16[256,1024]{0,1:T(8,128)(2,1)S(1)} %all_gather.7) | copy-start | bytes 1572868
  22.2 17.2 %collective-permute-start = (bf16[2,256,8,128]{3,1,2,0:T(8,128)(2,1)}, bf16[2,256,8,128]{3,1,2,0:T(8,128)(2,1)}, u32[]{:S(2)}, u32[]{:S(2)}) collective-permute-start(bf16[2,256,8,128]{3,1,2,0:T(8,128)(2,1)} %pad_maximum_fusion), channel_id=1, source_target_pairs={{0,2},{2,4},{4,6},{6,8},{8,10},{10,12},{12,14},{14,16},{16,18},{18... | collective-permute-start | bytes 3145736 | tf_op jit(solution)/shard_map/ppermute | solution.py:18
  39.5 17.1 %collective-permute-start.1 = (bf16[2,256,8,128]{3,1,2,0:T(8,128)(2,1)}, bf16[2,256,8,128]{3,1,2,0:T(8,128)(2,1)S(1)}, u32[]{:S(2)}, u32[]{:S(2)}) collective-permute-start(bf16[2,256,8,128]{3,1,2,0:T(8,128)(2,1)} %collective-permute-done), channel_id=1, source_target_pairs={{0,2},{2,4},{4,6},{6,8},{8,10},{10,12},{12,14},{14,16},{16,18},{18... | collective-permute-start | bytes 3145736 | tf_op jit(solution)/shard_map/ppermute | solution.py:18
  56.6 9.7 %copy-start.3 = (bf16[2,256,8,128]{3,1,2,0:T(8,128)(2,1)}, bf16[2,256,8,128]{3,1,2,0:T(8,128)(2,1)S(1)}, u32[]{:S(2)}) copy-start(bf16[2,256,8,128]{3,1,2,0:T(8,128)(2,1)S(1)} %collective-permute-done.1) | copy-start | bytes 3145732
  56.6 16.9 %collective-permute-start.2 = (bf16[2,256,8,128]{3,1,2,0:T(8,128)(2,1)S(1)}, bf16[2,256,8,128]{3,1,2,0:T(8,128)(2,1)S(1)}, u32[]{:S(2)}, u32[]{:S(2)}) collective-permute-start(bf16[2,256,8,128]{3,1,2,0:T(8,128)(2,1)S(1)} %collective-permute-done.1), channel_id=1, source_target_pairs={{0,2},{2,4},{4,6},{6,8},{8,10},{10,12},{12,14},{14,16},{16,18},{18... | collective-permute-start | bytes 3145736 | tf_op jit(solution)/shard_map/ppermute | solution.py:18
  66.3 13.7 %copy-start.2 = (bf16[256,1024]{0,1:T(8,128)(2,1)S(1)}, bf16[256,1024]{0,1:T(8,128)(2,1)}, u32[]{:S(2)}) copy-start(bf16[256,1024]{0,1:T(8,128)(2,1)} %copy-done.1) | copy-start | bytes 1572868
  73.5 6.5 %copy-start.5 = (bf16[2,256,8,128]{3,1,2,0:T(8,128)(2,1)}, bf16[2,256,8,128]{3,1,2,0:T(8,128)(2,1)S(1)}, u32[]{:S(2)}) copy-start(bf16[2,256,8,128]{3,1,2,0:T(8,128)(2,1)S(1)} %collective-permute-done.2) | copy-start | bytes 3145732
  101.3 10.1 %copy-start.4 = (bf16[2,256,8,128]{3,1,2,0:T(8,128)(2,1)S(1)}, bf16[2,256,8,128]{3,1,2,0:T(8,128)(2,1)}, u32[]{:S(2)}) copy-start(bf16[2,256,8,128]{3,1,2,0:T(8,128)(2,1)} %copy-done.3) | copy-start | bytes 3145732
  101.3 14.3 %slice-start = ((s8[6291456]{0:T(1024)(128)(4,1)}), s8[4194304]{0:T(1024)(128)(4,1)S(1)}, s32[]{:S(2)}) async-start(s8[6291456]{0:T(1024)(128)(4,1)} %bitcast.153), calls=%async_computation | async-start | bytes 8388608
  111.4 4.3 %slice-start.1 = ((s8[6291456]{0:T(1024)(128)(4,1)}), s8[2097152]{0:T(1024)(128)(4,1)S(1)}, s32[]{:S(2)}) async-start(s8[6291456]{0:T(1024)(128)(4,1)} %bitcast.153), calls=%async_computation.1 | async-start | bytes 4194304
  111.4 4.3 %copy-start.6 = (bf16[2,256,8,128]{3,1,2,0:T(8,128)(2,1)S(1)}, bf16[2,256,8,128]{3,1,2,0:T(8,128)(2,1)}, u32[]{:S(2)}) copy-start(bf16[2,256,8,128]{3,1,2,0:T(8,128)(2,1)} %copy-done.5) | copy-start | bytes 3145732
where the time goes:
time: 129 us
  matrix products  48.4 us (38%)
  waiting for transfers between devices  28.1 us (22%)
  other arithmetic  19.6 us (15%)
  blocking collectives  18.2 us (14%)
  local copies, waits for them, and re-layouts  9.24 us (7%)
  between operations  5.47 us (4%)
    dot_general x4, matrix products, advance(): jnp.einsum('tkgs,skd->tkgd', weights, value_block, preferred_element_type...  29.3 us
    ppermute x3, waiting for transfers between devices, passed_along(): return lax.ppermute(value, axis, pairs)  28.1 us
    dot_general x4, matrix products, advance(): jnp.einsum('tkgd,skd->tkgs', queries_h, key_block, preferred_element_type...  19.1 us
    reduce_sum x2, other arithmetic, advance(): running_sum = running_sum * rescale + jnp.sum(exp_scores, axis=-1)  16.8 us
    all_gather x1, blocking collectives, per_device(): lax.all_gather(keys, 'tp', axis=0, tiled=True)  10 us
    all_gather x1, blocking collectives, per_device(): lax.all_gather(values, 'tp', axis=0, tiled=True)  8.17 us
    unnamed x21, local copies, waits for them, and re-layouts  5.92 us
    reshape x1, local copies, waits for them, and re-layouts, per_device(): attended = attended.reshape(token_rows, kv_local * group_size * HD)  2.77 us
  transfers between devices with their start and end apart: 3, of which 3 were waited for; matrix products, arithmetic and copies ran while one was open for 14% of the time, Pallas kernels for 0%

commit v1 on v0

--- a/solution.py
+++ b/solution.py
@@ -1,8 +1,11 @@
+import functools
 import math
 
 import jax
 import jax.numpy as jnp
 from jax import lax
+from jax.experimental import pallas as pl
+from jax.experimental.pallas import tpu as pltpu
 from jax.sharding import PartitionSpec as P
 
 HD = 128
@@ -65,7 +68,7 @@
     return final_state
 
 
-def per_device(queries, keys, values, block_order):
+def general_device(queries, keys, values, block_order):
     block_total = block_order.shape[0]
     ctx_index = lax.axis_index("ctx")
     local_k, local_v = (
@@ -102,7 +105,192 @@
     return attended
 
 
+ROW_BLOCK = 4
+
+
+def scored(left, right):
+    return lax.dot_general(
+        left, right, (((1,), (1,)), ((), ())), preferred_element_type=jnp.float32
+    )
+
+
+def weighed(left, right):
+    return lax.dot_general(
+        left, right, (((1,), (0,)), ((), ())), preferred_element_type=jnp.float32
+    )
+
+
+def attention_kernel(bias_ref, queries_ref, *refs, tiles, group, own, first, last):
+    pairs, refs = refs[:tiles], refs[tiles:]
+    if not first:
+        (sum_in, stat_in), refs = refs[:2], refs[2:]
+    rows = queries_ref.shape[0]
+    scale = math.log2(math.e) / math.sqrt(HD)
+    key_rows = jnp.concatenate([pair[:rows] for pair in pairs], axis=0)
+    value_cols = jnp.concatenate([pair[rows:].T for pair in pairs], axis=1)
+    value_cols = jnp.concatenate(
+        [value_cols, jnp.ones((16, value_cols.shape[1]), jnp.bfloat16)], axis=0
+    )
+    if own:
+        key_ids = lax.broadcasted_iota(jnp.int32, (rows, rows), 0)
+        row_ids = lax.broadcasted_iota(jnp.int32, (rows, rows), 1)
+        causal = jnp.where(key_ids <= row_ids, 0.0, MASKED_SCORE).astype(jnp.float32)
+        causal = jnp.concatenate([causal] * ROW_BLOCK, axis=1)
+
+    def span(head):
+        return slice(head * rows, (head + ROW_BLOCK) * rows)
+
+    def scores(head):
+        block = jnp.concatenate(
+            [queries_ref[:, (head + i) * HD : (head + i + 1) * HD] for i in range(ROW_BLOCK)], axis=0
+        )
+        product = scored(key_rows, block)
+        parts = [
+            product[t * rows : (t + 1) * rows] + (causal if own and t == 0 else bias_ref[t])
+            for t in range(tiles)
+        ]
+        top = parts[0]
+        for part in parts[1:]:
+            top = jnp.maximum(top, part)
+        top = jnp.max(top, axis=0, keepdims=True)
+        if not first:
+            top = jnp.maximum(top, stat_in[0:1, span(head)])
+        return parts, top
+
+    def finish(head, parts, top):
+        weights = jnp.concatenate(
+            [jnp.exp2((part - top) * scale).astype(jnp.bfloat16) for part in parts], axis=0
+        )
+        product = weighed(value_cols, weights)
+        total, numerator = product[HD : HD + 1], product[:HD]
+        if not first:
+            rescale = jnp.exp2((stat_in[0:1, span(head)] - top) * scale)
+            total = total + stat_in[1:2, span(head)] * rescale
+            numerator = numerator + sum_in[:, span(head)] * rescale
+        if last:
+            (out_ref,) = refs
+            result = (numerator / total).T.astype(jnp.bfloat16)
+            for i in range(ROW_BLOCK):
+                out_ref[:, (head + i) * HD : (head + i + 1) * HD] = result[i * rows : (i + 1) * rows]
+        else:
+            sum_out, stat_out = refs
+            sum_out[:, span(head)] = numerator
+            stat_out[0:1, span(head)] = top
+            stat_out[1:2, span(head)] = total
+
+    heads = list(range(0, group, ROW_BLOCK))
+    ahead = scores(heads[0])
+    for index, head in enumerate(heads):
+        now = ahead
+        if index + 1 < len(heads):
+            ahead = scores(heads[index + 1])
+        finish(head, *now)
+
+
+def attend(bias, queries, pairs, state, own, last):
+    rows, width = queries.shape
+    kv_local = pairs[0].shape[1] // HD
+    group = width // (HD * kv_local)
+    tiles = len(pairs)
+    queries_spec = pl.BlockSpec((rows, group * HD), lambda h, b: (0, h))
+    pair_spec = pl.BlockSpec((2 * rows, HD), lambda h, b: (0, h))
+    sum_spec = pl.BlockSpec((HD, group * rows), lambda h, b: (0, h))
+    stat_spec = pl.BlockSpec((8, group * rows), lambda h, b: (0, h))
+    in_specs = [queries_spec] + [pair_spec] * tiles
+    if state is not None:
+        in_specs += [sum_spec, stat_spec]
+    if last:
+        out_specs = queries_spec
+        out_shape = jax.ShapeDtypeStruct(queries.shape, jnp.bfloat16)
+    else:
+        out_specs = (sum_spec, stat_spec)
+        out_shape = tuple(
+            jax.ShapeDtypeStruct((depth, kv_local * group * rows), jnp.float32) for depth in (HD, 8)
+        )
+    score_count = kv_local * group * rows * rows * tiles
+    return pl.pallas_call(
+        functools.partial(
+            attention_kernel,
+            tiles=tiles, group=group, own=own, first=state is None, last=last,
+        ),
+        grid_spec=pltpu.PrefetchScalarGridSpec(
+            num_scalar_prefetch=1, grid=(kv_local,), in_specs=in_specs, out_specs=out_specs
+        ),
+        out_shape=out_shape,
+        cost_estimate=pl.CostEstimate(
+            flops=4 * score_count * HD,
+            bytes_accessed=4 * rows * width * 2,
+            transcendentals=score_count,
+        ),
+    )(bias, queries, *pairs, *(state or ()))
+
+
+def span_device(queries, keys, values, block_order):
+    block_total = block_order.shape[0]
+    ctx_index = lax.axis_index("ctx")
+    tp_index = lax.axis_index("tp")
+
+    def moved(value, target):
+        pairs = []
+        for block in range(block_total):
+            for half in range(2):
+                to_block, to_half = target(block, half)
+                pairs.append((block * 2 + half, (to_block % block_total) * 2 + to_half))
+        return lax.ppermute(value, ("ctx", "tp"), pairs)
+
+    def across(block, half):
+        return block, 1 - half
+
+    def two_on(block, half):
+        return block + 2, half
+
+    def to_next_pair(block, half):
+        return block + (3 if block % 2 else 1), half
+
+    def swapped(block, half):
+        return block ^ 1, half
+
+    own = jnp.concatenate([keys, values], axis=0)
+    other_0 = moved(own, across)
+    same_2 = moved(own, two_on)
+    same_a = moved(own, to_next_pair)
+    other_2 = moved(same_2, across)
+    same_b = moved(same_2, swapped)
+    other_a = moved(other_0, to_next_pair)
+    other_b = moved(other_2, swapped)
+
+    even = ctx_index % 2 == 0
+    step_a = jnp.where(even, 3, 1)
+    step_b = jnp.where(even, 1, 3)
+
+    def position(step, half):
+        leading = block_order[(ctx_index - step) % block_total]
+        return jnp.where(half == 0, leading, 2 * block_total - 1 - leading)
+
+    query_span = position(0, tp_index)
+    tiles = [
+        (0, 0), (0, 1), (2, 0), (step_a, 0),
+        (step_b, 0), (step_a, 1), (2, 1), (step_b, 1),
+    ]
+    spans = jnp.stack(
+        [position(step, tp_index if flip == 0 else 1 - tp_index) for step, flip in tiles]
+    )
+    bias = jnp.where(spans < query_span, 0.0, MASKED_SCORE).astype(jnp.float32)
+    state = attend(bias[:4], queries, [own, other_0, same_2, same_a], None, True, False)
+    return attend(bias[4:], queries, [same_b, other_a, other_2, other_b], state, False, True)
+
+
 def solution(mesh):
+    block_total, halves = mesh.shape["ctx"], mesh.shape["tp"]
+
+    def per_device(queries, keys, values, block_order):
+        rows = queries.shape[0]
+        group = queries.shape[1] // keys.shape[1]
+        fits = halves == 2 and block_total % 2 == 0 and block_total > PREV and rows == HD
+        if fits and group % ROW_BLOCK == 0 and block_order.shape[0] == block_total:
+            return span_device(queries, keys, values, block_order)
+        return general_device(queries, keys, values, block_order)
+
     return jax.shard_map(
         per_device,
         mesh=mesh,

time: 129 us -> 62.5 us (0.48)
  matrix products: 48.4 us -> 0 us
  Pallas kernels: 0 us -> 26.7 us
  other arithmetic: 19.6 us -> 0.01 us
  blocking collectives: 18.2 us -> 0 us
  waiting for transfers between devices: 28.1 us -> 15.6 us
  starting transfers between devices: 0.01 us -> 6.62 us
  local copies, waits for them, and re-layouts: 9.24 us -> 5.36 us
  between operations: 5.47 us -> 7.41 us
    dot_general x8 -> x0, matrix products: 48.4 us -> none  [the longest x4 29.3 us: advance(): jnp.einsum('tkgs,skd->tkgd', weights, value_block, preferred_element_type...]
    pallas_call x0 -> x2, Pallas kernels: none -> 26.7 us  [attend(): pl.pallas_call(functools.partial(attention_kernel, tiles=tiles, group=gro...]
    all_gather x2 -> x0, blocking collectives: 18.2 us -> none  [the longest x1 10 us: per_device(): lax.all_gather(keys, 'tp', axis=0, tiled=True)]
    reduce_sum x3 -> x0, other arithmetic: 18.2 us -> none  [the longest x2 16.8 us: advance(): running_sum = running_sum * rescale + jnp.sum(exp_scores, axis=-1)]
    ppermute x3 -> x7, waiting for transfers between devices: 28.1 us -> 15.6 us  [moved(): return lax.ppermute(value, ('ctx', 'tp'), pairs)]
    ppermute x3 -> x7, starting transfers between devices: 0.01 us -> 6.62 us  [moved(): return lax.ppermute(value, ('ctx', 'tp'), pairs)]
    unnamed x21 -> x13, local copies, waits for them, and re-layouts: 5.92 us -> 2.1 us
    reshape x1 -> x0, local copies, waits for them, and re-layouts: 2.77 us -> none  [per_device(): attended = attended.reshape(token_rows, kv_local * group_size * HD)]
  transfers between devices with their start and end apart: 3 -> 7, of which waited for: 3 -> 2; matrix products, arithmetic and copies ran while one was open for 14% -> 4% of each run, Pallas kernels for 0% -> 21%
where the time goes in v1:
time: 62.5 us; the launch traced here: 61.7 us
  Pallas kernels  26.7 us (43%)
  waiting for transfers between devices  15.6 us (25%)
  between operations  7.41 us (12%)
  starting transfers between devices  6.62 us (11%)
  local copies, waits for them, and re-layouts  5.36 us (9%)
    pallas_call x2, Pallas kernels, attend(): pl.pallas_call(functools.partial(attention_kernel, tiles=tiles, group=gro...  26.7 us
    ppermute x7, waiting for transfers between devices, moved(): return lax.ppermute(value, ('ctx', 'tp'), pairs)  15.6 us
    ppermute x7, starting transfers between devices, moved(): return lax.ppermute(value, ('ctx', 'tp'), pairs)  6.62 us
    unnamed x13, local copies, waits for them, and re-layouts  2.1 us
    dynamic_slice x1, local copies, waits for them, and re-layouts, position(): leading = block_order[(ctx_index - step) % block_total]  1.46 us
  transfers between devices with their start and end apart: 7, of which 2 were waited for; matrix products, arithmetic and copies ran while one was open for 4% of the time, Pallas kernels for 21%

profile of v1, /device:TPU:0, one launch (start us, length us, event | category | flops | bytes accessed | tf_op | source)
XLA Modules:
  0.0 61.7 jit_solution(9678880634553379999)
XLA Ops:
  0.0 1.0 %constant_dynamic-update-slice_fusion.1 = bf16[256,1024]{1,0:T(8,128)(2,1)S(1)} fusion(bf16[128,1024]{1,0:T(8,128)(2,1)} %param.5), kind=kLoop, calls=%fused_computation.1 | loop fusion | bytes 524288
  1.0 1.0 %constant_dynamic-update-slice_fusion.refs_0_ = bf16[256,1024]{1,0:T(8,128)(2,1)S(1)} fusion(bf16[256,1024]{1,0:T(8,128)(2,1)S(1)} %constant_dynamic-update-slice_fusion.1, bf16[128,1024]{1,0:T(8,128)(2,1)} %param.6), kind=kLoop, calls=%fused_computation | loop fusion | bytes 524288 | tf_op jit(solution)/shard_map/concatenate | solution.py:253
  1.9 0.0 copy-start.4
  2.0 3.0 %collective-permute-start = (bf16[256,1024]{1,0:T(8,128)(2,1)S(1)}, bf16[256,1024]{1,0:T(8,128)(2,1)S(1)}, u32[]{:S(2)}, u32[]{:S(2)}) collective-permute-start(bf16[256,1024]{1,0:T(8,128)(2,1)S(1)} %constant_dynamic-update-slice_fusion.refs_0_), channel_id=1, source_target_pairs={{0,4},{1,5},{2,6},{3,7},{4,8},{5,9},{6,10},{7,11},{8,12},{9,13},{1... | collective-permute-start | bytes 1572872 | tf_op jit(solution)/shard_map/ppermute | solution.py:239
  5.0 1.5 %collective-permute-start.2 = (bf16[256,1024]{1,0:T(8,128)(2,1)S(1)}, bf16[256,1024]{1,0:T(8,128)(2,1)}, u32[]{:S(2)}, u32[]{:S(2)}) collective-permute-start(bf16[256,1024]{1,0:T(8,128)(2,1)S(1)} %constant_dynamic-update-slice_fusion.refs_0_), channel_id=1, source_target_pairs={{0,1},{1,0},{2,3},{3,2},{4,5},{5,4},{6,7},{7,6},{8,9},{9,8},{10,11... | collective-permute-start | bytes 1572872 | tf_op jit(solution)/shard_map/ppermute | solution.py:239
  6.5 13.4 %collective-permute-done.refs_2_ = bf16[256,1024]{1,0:T(8,128)(2,1)S(1)} collective-permute-done((bf16[256,1024]{1,0:T(8,128)(2,1)S(1)}, bf16[256,1024]{1,0:T(8,128)(2,1)S(1)}, u32[]{:S(2)}, u32[]{:S(2)}) %collective-permute-start) | collective-permute-done | bytes 524320 | tf_op jit(solution)/shard_map/ppermute | solution.py:239
  19.9 1.5 %collective-permute-start.4 = (bf16[256,1024]{1,0:T(8,128)(2,1)S(1)}, bf16[256,1024]{1,0:T(8,128)(2,1)S(1)}, u32[]{:S(2)}, u32[]{:S(2)}) collective-permute-start(bf16[256,1024]{1,0:T(8,128)(2,1)S(1)} %collective-permute-done.refs_2_), channel_id=1, source_target_pairs={{0,1},{1,0},{2,3},{3,2},{4,5},{5,4},{6,7},{7,6},{8,9},{9,8},{10,11... | collective-permute-start | bytes 1572872 | tf_op jit(solution)/shard_map/ppermute | solution.py:239
  21.5 0.0 collective-permute-start.6
  21.5 1.5 %fusion.1 = (s32[1]{0:T(128)}, s32[1]{0:T(128)}, s32[1]{0:T(128)}, s32[1]{0:T(128)}) fusion(s32[16]{0:T(128)} %param.7, s32[]{:T(128)S(6)} %select_n.100, s32[]{:T(128)S(6)} %select_n.91, s32[]{:T(128)S(6)} %select_n.87, s32[]{:T(128)S(6)} %select_n.96), kind=kLoop, calls=%fused_computation.4 | loop fusion | bytes 48 | tf_op jit(solution)/shard_map/dynamic_slice | solution.py:267
  30.2 0.1 stack.35
  30.3 0.1 collective-permute-start.1
  30.4 0.0 collective-permute-done.2.refs_1_
  30.4 0.5 collective-permute-start.3
  30.9 2.1 %collective-permute-done.4.refs_2_ = bf16[256,1024]{1,0:T(8,128)(2,1)S(1)} collective-permute-done((bf16[256,1024]{1,0:T(8,128)(2,1)S(1)}, bf16[256,1024]{1,0:T(8,128)(2,1)S(1)}, u32[]{:S(2)}, u32[]{:S(2)}) %collective-permute-start.4) | collective-permute-done | bytes 524320 | tf_op jit(solution)/shard_map/ppermute | solution.py:239
  33.0 0.0 copy-start
  33.0 0.0 collective-permute-start.5
  33.0 0.7 %fusion = (f32[4]{0:T(128)}, f32[4]{0:T(128)}) fusion(f32[8]{0:T(128)S(1)} %compare_select_fusion), kind=kLoop, calls=%fused_computation.3 | loop fusion | bytes 64 | tf_op jit(solution)/shard_map/slice | solution.py:279
  33.8 0.0 collective-permute-done.6.refs_3_
  33.8 0.0 copy-done.4
  33.8 0.0 copy-done.5
  33.8 12.7 %shard_map.46 = (f32[128,12288]{1,0:T(8,128)}, f32[8,12288]{1,0:T(8,128)}) custom-call(f32[4]{0:T(128)} %get-tuple-element.9.bias_ref, bf16[128,12288]{1,0:T(8,128)(2,1)} %queries_ref.3, bf16[256,1024]{1,0:T(8,128)(2,1)} %copy-done.4, bf16[256,1024]{1,0:T(8,128)(2,1)} %collective-permute-done.2.refs_1_, bf16[256,1024]{1,0:T(8,128)(2,1)} %copy-done.5, ...), custom_call_target="tpu_custom_call" | custom-call | flops 3221225472 | bytes 12582912 | tf_op jit(solution)/shard_map/pallas_call | solution.py:211
  46.5 0.0 copy-done
  46.5 0.0 collective-permute-done.3.refs_1_
  46.5 0.0 copy-start.2
  46.5 0.0 collective-permute-done.1.refs_0_
  46.6 0.0 copy-start.1
  46.6 0.0 collective-permute-done.5.refs_3_
  46.6 0.0 copy-start.3
  46.6 0.7 %copy-done.2 = bf16[256,1024]{1,0:T(8,128)(2,1)} copy-done((bf16[256,1024]{1,0:T(8,128)(2,1)}, bf16[256,1024]{1,0:T(8,128)(2,1)S(1)}, u32[]{:S(2)}) %copy-start.2) | copy-done | bytes 524312
  47.3 0.2 copy-done.1
  47.6 0.1 copy-done.3
  47.7 14.0 %shard_map.47 = bf16[128,12288]{1,0:T(8,128)(2,1)} custom-call(f32[4]{0:T(128)} %get-tuple-element.10.bias_ref, bf16[128,12288]{1,0:T(8,128)(2,1)} %queries_ref.3, bf16[256,1024]{1,0:T(8,128)(2,1)} %copy-done.1, bf16[256,1024]{1,0:T(8,128)(2,1)} %copy-done.2, bf16[256,1024]{1,0:T(8,128)(2,1)} %copy-done, bf16[256,1024]{1,0:T(8,128)(2,1)} %copy-done.3, ...), custom_call_target="tpu_custom_call" | custom-call | flops 3221225472 | bytes 12582912 | tf_op jit(solution)/shard_map/pallas_call | solution.py:211
  (2 shorter events, 0.0 us)
Async XLA Ops:
  1.9 31.8 %copy-start.4 = (bf16[256,1024]{1,0:T(8,128)(2,1)}, bf16[256,1024]{1,0:T(8,128)(2,1)S(1)}, u32[]{:S(2)}) copy-start(bf16[256,1024]{1,0:T(8,128)(2,1)S(1)} %constant_dynamic-update-slice_fusion.refs_0_) | copy-start | bytes 1572868
  2.0 18.0 %collective-permute-start = (bf16[256,1024]{1,0:T(8,128)(2,1)S(1)}, bf16[256,1024]{1,0:T(8,128)(2,1)S(1)}, u32[]{:S(2)}, u32[]{:S(2)}) collective-permute-start(bf16[256,1024]{1,0:T(8,128)(2,1)S(1)} %constant_dynamic-update-slice_fusion.refs_0_), channel_id=1, source_target_pairs={{0,4},{1,5},{2,6},{3,7},{4,8},{5,9},{6,10},{7,11},{8,12},{9,13},{1... | collective-permute-start | bytes 1572872 | tf_op jit(solution)/shard_map/ppermute | solution.py:239
  5.0 25.4 %collective-permute-start.2 = (bf16[256,1024]{1,0:T(8,128)(2,1)S(1)}, bf16[256,1024]{1,0:T(8,128)(2,1)}, u32[]{:S(2)}, u32[]{:S(2)}) collective-permute-start(bf16[256,1024]{1,0:T(8,128)(2,1)S(1)} %constant_dynamic-update-slice_fusion.refs_0_), channel_id=1, source_target_pairs={{0,1},{1,0},{2,3},{3,2},{4,5},{5,4},{6,7},{7,6},{8,9},{9,8},{10,11... | collective-permute-start | bytes 1572872 | tf_op jit(solution)/shard_map/ppermute | solution.py:239
  19.9 13.9 %copy-start.5 = (bf16[256,1024]{1,0:T(8,128)(2,1)}, bf16[256,1024]{1,0:T(8,128)(2,1)S(1)}, u32[]{:S(2)}) copy-start(bf16[256,1024]{1,0:T(8,128)(2,1)S(1)} %collective-permute-done.refs_2_) | copy-start | bytes 1572868
  19.9 13.1 %collective-permute-start.4 = (bf16[256,1024]{1,0:T(8,128)(2,1)S(1)}, bf16[256,1024]{1,0:T(8,128)(2,1)S(1)}, u32[]{:S(2)}, u32[]{:S(2)}) collective-permute-start(bf16[256,1024]{1,0:T(8,128)(2,1)S(1)} %collective-permute-done.refs_2_), channel_id=1, source_target_pairs={{0,1},{1,0},{2,3},{3,2},{4,5},{5,4},{6,7},{7,6},{8,9},{9,8},{10,11... | collective-permute-start | bytes 1572872 | tf_op jit(solution)/shard_map/ppermute | solution.py:239
  21.5 12.3 %collective-permute-start.6 = (bf16[256,1024]{1,0:T(8,128)(2,1)S(1)}, bf16[256,1024]{1,0:T(8,128)(2,1)}, u32[]{:S(2)}, u32[]{:S(2)}) collective-permute-start(bf16[256,1024]{1,0:T(8,128)(2,1)S(1)} %constant_dynamic-update-slice_fusion.refs_0_), channel_id=1, source_target_pairs={{0,2},{1,3},{2,8},{3,9},{4,6},{5,7},{6,12},{7,13},{8,10},{9,11},{1... | collective-permute-start | bytes 1572872 | tf_op jit(solution)/shard_map/ppermute | solution.py:239
  30.3 16.2 %collective-permute-start.1 = (bf16[256,1024]{1,0:T(8,128)(2,1)S(1)}, bf16[256,1024]{1,0:T(8,128)(2,1)S(1)}, u32[]{:S(2)}, u32[]{:S(2)}) collective-permute-start(bf16[256,1024]{1,0:T(8,128)(2,1)S(1)} %collective-permute-done.refs_2_), channel_id=1, source_target_pairs={{0,2},{1,3},{2,0},{3,1},{4,6},{5,7},{6,4},{7,5},{8,10},{9,11},{10,... | collective-permute-start | bytes 1572872 | tf_op jit(solution)/shard_map/ppermute | solution.py:239
  30.4 16.1 %collective-permute-start.3 = (bf16[256,1024]{1,0:T(8,128)(2,1)}, bf16[256,1024]{1,0:T(8,128)(2,1)S(1)}, u32[]{:S(2)}, u32[]{:S(2)}) collective-permute-start(bf16[256,1024]{1,0:T(8,128)(2,1)} %collective-permute-done.2.refs_1_), channel_id=1, source_target_pairs={{0,2},{1,3},{2,8},{3,9},{4,6},{5,7},{6,12},{7,13},{8,10},{9,11},{1... | collective-permute-start | bytes 1572872 | tf_op jit(solution)/shard_map/ppermute | solution.py:239
  33.0 13.5 %copy-start = (bf16[256,1024]{1,0:T(8,128)(2,1)}, bf16[256,1024]{1,0:T(8,128)(2,1)S(1)}, u32[]{:S(2)}) copy-start(bf16[256,1024]{1,0:T(8,128)(2,1)S(1)} %collective-permute-done.4.refs_2_) | copy-start | bytes 1572868
  33.0 13.5 %collective-permute-start.5 = (bf16[256,1024]{1,0:T(8,128)(2,1)S(1)}, bf16[256,1024]{1,0:T(8,128)(2,1)S(1)}, u32[]{:S(2)}, u32[]{:S(2)}) collective-permute-start(bf16[256,1024]{1,0:T(8,128)(2,1)S(1)} %collective-permute-done.4.refs_2_), channel_id=1, source_target_pairs={{0,2},{1,3},{2,0},{3,1},{4,6},{5,7},{6,4},{7,5},{8,10},{9,11},{10,... | collective-permute-start | bytes 1572872 | tf_op jit(solution)/shard_map/ppermute | solution.py:239
  46.5 0.8 %copy-start.2 = (bf16[256,1024]{1,0:T(8,128)(2,1)}, bf16[256,1024]{1,0:T(8,128)(2,1)S(1)}, u32[]{:S(2)}) copy-start(bf16[256,1024]{1,0:T(8,128)(2,1)S(1)} %collective-permute-done.3.refs_1_) | copy-start | bytes 1572868
  46.6 1.0 %copy-start.1 = (bf16[256,1024]{1,0:T(8,128)(2,1)}, bf16[256,1024]{1,0:T(8,128)(2,1)S(1)}, u32[]{:S(2)}) copy-start(bf16[256,1024]{1,0:T(8,128)(2,1)S(1)} %collective-permute-done.1.refs_0_) | copy-start | bytes 1572868
  46.6 1.1 %copy-start.3 = (bf16[256,1024]{1,0:T(8,128)(2,1)}, bf16[256,1024]{1,0:T(8,128)(2,1)S(1)}, u32[]{:S(2)}) copy-start(bf16[256,1024]{1,0:T(8,128)(2,1)S(1)} %collective-permute-done.5.refs_3_) | copy-start | bytes 1572868
